TPU v7x, 512 devices: a whole 4x8x8 slice. The times are simulated.
512 devices in a mesh: row: 32 (over y, x), col: 16 (over z, core).
Axes of the slice: x: 4, y: 8, z: 8, core: 2. Of those that a mesh axis runs over, the one named last changes fastest.
Arguments:
- weights: bfloat16 [8192, 8192], P('row', 'col'), may hold values from 0.0099487305 to 1
- tile_mask: int32 [64, 64], P('row', 'col'), may hold values from 0 to 1, as said below
Outputs:
- flow: float32 [8192, 8192], P('row', 'col')
Inputs may be any that keep to these rules, and one draw needn't show every extreme that they name: `tile_mask`: each column of tiles holds exactly 8 ones, the diagonal tile among them.
All inputs are finite; a program needn't handle non-finite values.
Results may differ from a plain program's by a relative error of at most 0.00095.
Values may be sent and summed in bfloat16 or wider, within the bound.
A program may use at most 64 MiB of HBM per device.

v0:
```python
import jax
import jax.numpy as jnp
from jax import lax
from jax.sharding import PartitionSpec as P

KEEP = 8


def from_everyone(shard, axis):
    copies = jnp.broadcast_to(shard, (lax.axis_size(axis), *shard.shape))
    return lax.all_to_all(copies, axis, split_axis=0, concat_axis=0, tiled=True)


def of_everyone(shard, axis):
    return from_everyone(shard, axis).sum(axis=0)


def laid_out(tiles, dim):
    shape = list(tiles.shape[1:])
    shape[dim] *= tiles.shape[0]
    return jnp.moveaxis(tiles, 0, dim).reshape(shape)


def collect(shard, axis, dim):
    tiles = from_everyone(shard, axis)
    return laid_out(tiles, dim)


def cut_along(shard, dim, size):
    before, after = (shard.shape[:dim], shard.shape[dim + 1 :])
    return jnp.moveaxis(shard.reshape(*before, size, -1, *after), dim, 0)


def sum_at_owner(shard, axis, dim):
    tiles = cut_along(shard, dim, lax.axis_size(axis))
    arrived = lax.all_to_all(tiles, axis, split_axis=0, concat_axis=0, tiled=True)
    return arrived.astype(jnp.float32).sum(axis=0)


def filled_up(lines, size):
    spare = -lines.shape[0] % size
    if not spare:
        return lines
    return jnp.concatenate([lines, jnp.zeros((spare, *lines.shape[1:]), lines.dtype)])


def total_of(shard, axes):
    lines = shard.reshape(-1, shard.shape[-1])
    own = sum_at_owner(filled_up(lines, lax.axis_size(axes)), axes, 0)
    whole = collect(own.astype(jnp.bfloat16), axes, 0)
    return whole[: len(lines)].reshape(shard.shape).astype(jnp.float32)


def on_device(weights, tile_mask):
    tile_rows, tile_cols = tile_mask.shape
    row_count, col_count = weights.shape
    tile_size = row_count // tile_rows
    shaped = weights.astype(jnp.float32).reshape(tile_rows, tile_size, tile_cols, tile_size)
    masked = (shaped * tile_mask.astype(jnp.float32)[:, None, :, None]).reshape(
        row_count, col_count
    )
    degree = of_everyone(jnp.sum(masked, axis=0), "row")
    markov = (masked / degree[None, :]).astype(jnp.bfloat16)
    column_mask = collect(tile_mask, "row", 0)
    all_tiles = column_mask.shape[0]
    rank = jnp.cumsum(column_mask, axis=0) - column_mask
    slots = lax.broadcasted_iota(jnp.int32, (all_tiles, tile_cols, KEEP), 2)
    chosen = jnp.logical_and(column_mask[:, :, None] == 1, rank[:, :, None] == slots).astype(
        jnp.int32
    )
    tile_ids = lax.broadcasted_iota(jnp.int32, (all_tiles, tile_cols, KEEP), 0)
    source_ids = jnp.sum(tile_ids * chosen, axis=0)
    base = lax.axis_index("row") * tile_rows
    own_slots = lax.dynamic_slice_in_dim(chosen, base, tile_rows, 0).astype(jnp.bfloat16)
    local_tiles = markov.reshape(tile_rows, tile_size, tile_cols, tile_size)
    placed = jnp.einsum(
        "lcs,lacb->csab", own_slots, local_tiles, preferred_element_type=jnp.float32
    )
    gathered_tiles = total_of(placed.astype(jnp.bfloat16), "row").astype(jnp.bfloat16)
    left_panel = lax.all_gather(markov, "col", axis=1, tiled=True)
    left_tiles = left_panel.reshape(row_count, all_tiles, tile_size)
    selected = jnp.take(left_tiles, source_ids, axis=1)
    expanded = jnp.einsum(
        "rcsa,csab->rcb", selected, gathered_tiles, preferred_element_type=jnp.float32
    )
    expanded = expanded.reshape(row_count, col_count)
    inflated = expanded * expanded
    mass = of_everyone(jnp.sum(inflated, axis=0), "row")
    nodes = row_count * lax.axis_size("row")
    return inflated / mass[None, :] * nodes


def solution(mesh):
    placed = (P("row", "col"), P("row", "col"))
    return jax.shard_map(
        on_device, mesh=mesh, in_specs=placed, out_specs=P("row", "col"), check_vma=False
    )
```

profile of v0, /device:TPU:448, one launch (start us, length us, event | category | flops | bytes accessed | tf_op | source)
XLA Modules:
  0.0 133.4 jit_solution(13419072680064312521)
XLA Ops:
  6.5 0.8 convert_element_type.25
  7.3 0.1 copy.42
  7.4 1.1 copy.41
  8.5 0.2 mul.35
  8.7 0.1 fusion.11
  8.9 19.7 %all_to_all.27 = f32[32,1,512]{2,1,0:T(1,128)S(1)} all-to-all(f32[32,1,512]{2,1,0:T(1,128)S(1)} %broadcast_in_dim.29), channel_id=1, replica_groups=mesh['row'=32,'col'=16] {'row'}, dimensions={0} | all-to-all | bytes 131072 | tf_op jit(solution)/shard_map/all_to_all | solution.py:11
  28.7 0.8 divide_convert_fusion
  29.5 0.6 broadcast_in_dim.28
  30.2 3.8 %all-to-all-start = ((s32[32,2,4]{2,1,0:T(2,128)}), s32[32,2,4]{2,1,0:T(2,128)S(1)}, u32[]{:S(2)}, u32[]{:S(2)}) async-start(s32[32,2,4]{2,1,0:T(2,128)} %broadcast_in_dim.28), calls=%async_computation | async-start | bytes 65536 | tf_op jit(solution)/shard_map/all_to_all | solution.py:11
  34.0 9.8 %all-to-all-done = s32[32,2,4]{2,1,0:T(2,128)S(1)} async-done(((s32[32,2,4]{2,1,0:T(2,128)}), s32[32,2,4]{2,1,0:T(2,128)S(1)}, u32[]{:S(2)}, u32[]{:S(2)}) %all-to-all-start) | async-done | bytes 1056 | tf_op jit(solution)/shard_map/all_to_all | solution.py:11
  43.8 0.1 reduce_window_sum.11
  43.9 0.1 copy.39
  44.1 0.2 fusion.12
  44.2 1.0 reshape.64
  45.3 0.3 copy.44
  45.6 0.5 convolution_convert_fusion
  46.1 0.2 copy.45
  46.4 29.1 %all_to_all.28 = bf16[32,128,128]{2,1,0:T(8,128)(2,1)S(1)} all-to-all(bf16[32,128,128]{2,1,0:T(8,128)(2,1)S(1)} %bitcast.49), channel_id=1, replica_groups=mesh['row'=32,'col'=16] {'row'}, dimensions={0} | all-to-all | bytes 2097152 | tf_op jit(solution)/shard_map/all_to_all | solution.py:36
  75.4 0.2 reduce_sum.61
  75.6 0.1 copy.46
  75.7 1.3 broadcast_in_dim.30
  77.0 5.2 %all-to-all-start.3 = ((bf16[32,128,128]{1,2,0:T(8,128)(2,1)}), bf16[32,128,128]{1,2,0:T(8,128)(2,1)S(1)}, u32[]{:S(2)}, u32[]{:S(2)}) async-start(bf16[32,128,128]{1,2,0:T(8,128)(2,1)} %broadcast_in_dim.30), calls=%async_computation.3 | async-start | bytes 2097152 | tf_op jit(solution)/shard_map/all_to_all | solution.py:11
  82.3 0.1 select_reduce_fusion
  82.6 6.4 %copy.47 = bf16[256,64,128]{2,0,1:T(8,128)(2,1)} copy(bf16[256,64,128]{0,2,1:T(8,128)(2,1)} %bitcast.48) | data formatting | bytes 8388608 | tf_op jit(solution)/shard_map/reshape | solution.py:81
  88.9 3.1 %gather_fusion = bf16[32,256,128]{2,1,0:T(8,128)(2,1)S(1)} fusion(bf16[256,64,128]{2,0,1:T(8,128)(2,1)} %copy.47, s32[1024]{0:T(1024)S(1)} %pad_clamp_fusion), kind=kCustom, calls=%fused_computation | custom fusion | bytes 4194432 | tf_op jit(solution)/shard_map/jit(_take)/gather | solution.py:82
  92.1 15.9 %all-to-all-done.3 = bf16[32,128,128]{1,2,0:T(8,128)(2,1)S(1)} async-done(((bf16[32,128,128]{1,2,0:T(8,128)(2,1)}), bf16[32,128,128]{1,2,0:T(8,128)(2,1)S(1)}, u32[]{:S(2)}, u32[]{:S(2)}) %all-to-all-start.3) | async-done | bytes 1048608 | tf_op jit(solution)/shard_map/all_to_all | solution.py:11
  108.0 1.7 %fusion.18 = (f32[4,128]{1,0:T(4,128)S(1)}, f32[4,128,256]{2,1,0:T(8,128)}) fusion(bf16[4,8,128,128]{2,3,1,0:T(8,128)(2,1)S(1)} %bitcast.51, bf16[4,8,256,128]{3,2,1,0:T(8,128)(2,1)S(1)} %bitcast.50, pred[4,8]{1,0:T(4,128)(4,1)S(1)} %compare_and_fusion), kind=kOutput, calls=%fused_computation.26 | convolution fusion | flops 269745664 | bytes 3672096 | tf_op jit(solution)/shard_map/rcsa,csab->rcb/dot_general | solution.py:83
  109.6 0.7 broadcast_in_dim.34
  110.3 5.3 %all-to-all-start.4 = ((f32[32,1,512]{2,1,0:T(1,128)}), f32[32,1,512]{2,1,0:T(1,128)S(1)}, u32[]{:S(2)}, u32[]{:S(2)}) async-start(f32[32,1,512]{2,1,0:T(1,128)} %broadcast_in_dim.34), calls=%async_computation.4 | async-start | bytes 131072 | tf_op jit(solution)/shard_map/all_to_all | solution.py:11
  115.6 1.2 copy.49
  116.9 8.7 %all-to-all-done.4 = f32[32,1,512]{2,1,0:T(1,128)S(1)} async-done(((f32[32,1,512]{2,1,0:T(1,128)}), f32[32,1,512]{2,1,0:T(1,128)S(1)}, u32[]{:S(2)}, u32[]{:S(2)}) %all-to-all-start.4) | async-done | bytes 65568 | tf_op jit(solution)/shard_map/all_to_all | solution.py:11
  125.7 0.9 divide_multiply_fusion
  (15 shorter events, 0.4 us)
Async XLA Ops:
  6.5 23.0 %copy-start = (s32[2,4]{1,0:T(2,128)S(1)}, s32[2,4]{1,0:T(2,128)}, u32[]{:S(2)}) copy-start(s32[2,4]{1,0:T(2,128)} %param.3) | copy-start | bytes 100
  6.5 76.0 %all-gather.2.cloned.1.call-start = ((), (), s32[]{:S(2)}) async-start(), calls=%async_computation.5 | async-start | bytes 4456448 | tf_op jit(solution)/shard_map/all_gather | solution.py:80
  30.2 13.6 %all-to-all-start = ((s32[32,2,4]{2,1,0:T(2,128)}), s32[32,2,4]{2,1,0:T(2,128)S(1)}, u32[]{:S(2)}, u32[]{:S(2)}) async-start(s32[32,2,4]{2,1,0:T(2,128)} %broadcast_in_dim.28), calls=%async_computation | async-start | bytes 65536 | tf_op jit(solution)/shard_map/all_to_all | solution.py:11
  77.0 30.9 %all-to-all-start.3 = ((bf16[32,128,128]{1,2,0:T(8,128)(2,1)}), bf16[32,128,128]{1,2,0:T(8,128)(2,1)S(1)}, u32[]{:S(2)}, u32[]{:S(2)}) async-start(bf16[32,128,128]{1,2,0:T(8,128)(2,1)} %broadcast_in_dim.30), calls=%async_computation.3 | async-start | bytes 2097152 | tf_op jit(solution)/shard_map/all_to_all | solution.py:11
  110.3 15.3 %all-to-all-start.4 = ((f32[32,1,512]{2,1,0:T(1,128)}), f32[32,1,512]{2,1,0:T(1,128)S(1)}, u32[]{:S(2)}, u32[]{:S(2)}) async-start(f32[32,1,512]{2,1,0:T(1,128)} %broadcast_in_dim.34), calls=%async_computation.4 | async-start | bytes 131072 | tf_op jit(solution)/shard_map/all_to_all | solution.py:11
Sparse Core Ops, SparseCore 0:
  29.7 36.0 all-gather.1
where the time goes:
time: 134 us; the launch traced here: 133 us
  blocking collectives  48.8 us (36%)
  waiting for transfers between devices  34.4 us (26%)
  local copies, waits for them, and re-layouts  16.7 us (12%)
  starting transfers between devices  14.4 us (11%)
  between operations  13.5 us (10%)
  other arithmetic  3.34 us (2%)
  matrix products  2.2 us (2%)
    all_to_all x3, waiting for transfers between devices, from_everyone(): return lax.all_to_all(copies, axis, split_axis=0, concat_axis=0, tiled=True)  34.4 us
    all_to_all x1, blocking collectives, sum_at_owner(): lax.all_to_all(tiles, axis, split_axis=0, concat_axis=0, tiled=True)  29.1 us
    all_to_all x1, blocking collectives, from_everyone(): return lax.all_to_all(copies, axis, split_axis=0, concat_axis=0, tiled=True)  19.7 us
    all_to_all x3, starting transfers between devices, from_everyone(): return lax.all_to_all(copies, axis, split_axis=0, concat_axis=0, tiled=True)  14.4 us
    reshape x1, local copies, waits for them, and re-layouts, on_device(): left_tiles = left_panel.reshape(row_count, all_tiles, tile_size)  6.38 us
    gather x1, local copies, waits for them, and re-layouts, on_device(): selected = jnp.take(left_tiles, source_ids, axis=1)  3.14 us
  transfers between devices with their start and end apart: 4, of which 3 were waited for; matrix products, arithmetic and copies ran while one was open for 12% of the time, Pallas kernels for 0%

commit v1 on v0

v1 whole, which is shorter than its diff:
```python
import functools
import jax
import jax.numpy as jnp
from jax import lax
from jax.experimental import pallas as pl
from jax.experimental.pallas import tpu as pltpu
from jax.sharding import PartitionSpec as P

MESH = pl.DeviceIdType.MESH
KEEP = 8
CHIPS_X = 4
CORES = 2
SUBLANES, LANES = 8, 128


def kernel(
    size, rows, cols, mask_ref, w_ref, out_ref, scale_ref,
    block, left, stage, cand_out, cand, right, wide, inflated,
    xm, xd, ym, yd, xs, ys, inv, table, slots,
    s_xm, s_xd, s_ym, s_yd, s_xs, s_ys, s_inv, s_stage, s_cand, s_gy,
    s_gxp, s_gxm, s_rel, s_up, s_down, s_pair, s_local,
):
    nx, ny, nz = CHIPS_X, rows // CHIPS_X, cols // CORES
    tr, tc = block.shape[0] // size, block.shape[1] // size
    r, c = lax.axis_index("row"), lax.axis_index("col")
    x, y = lax.rem(r, nx), lax.div(r, nx)
    core, z = lax.rem(c, CORES), lax.div(c, CORES)
    sends = []

    def wrap(a, n):
        return lax.rem(a + n, n)

    def copy(src, dst, sem, out, arrive, row, col):
        return pltpu.make_async_remote_copy(
            src_ref=src, dst_ref=dst, send_sem=sem.at[0, out], recv_sem=sem.at[1, arrive],
            device_id=(row, col), device_id_type=MESH,
        )

    def send(*args):
        made = copy(*args)
        made.start()
        sends.append(made)

    def at_x(k):
        return y * nx + wrap(x + k, nx), c

    def at_y(k):
        return wrap(y + k, ny) * nx + x, c

    def at_col(k):
        return r, wrap(c + k, cols)

    barrier = pltpu.get_barrier_semaphore()
    partners = [at_x(k) for k in range(1, nx)] + [at_y(k) for k in range(1, ny)]
    partners += [at_col(k) for k in range(1, cols)]
    for partner in partners:
        pl.semaphore_signal(barrier, inc=1, device_id=partner, device_id_type=MESH)

    fetch = pltpu.make_async_copy(w_ref, block, s_local.at[0])
    fetch.start()
    lane = lax.broadcasted_iota(jnp.int32, (SUBLANES, LANES), 1)
    line = lax.broadcasted_iota(jnp.int32, (SUBLANES, LANES), 0)
    own_mask = jnp.zeros((SUBLANES, LANES), jnp.int32)
    for i in range(tr):
        for q in range(tc):
            here = jnp.logical_and(lane == r * tr + i, line == q)
            own_mask = jnp.where(here, mask_ref[i, q], own_mask)
    xm[x] = own_mask
    xs[x] = jnp.zeros((SUBLANES, LANES), jnp.float32)
    fetch.wait()
    degree = jnp.zeros((SUBLANES, LANES), jnp.float32)
    for q in range(tc):
        total = jnp.zeros((1, size), jnp.float32)
        for i in range(tr):
            tile = block[i * size : (i + 1) * size, q * size : (q + 1) * size]
            tile = tile.astype(jnp.float32) * mask_ref[i, q].astype(jnp.float32)
            total += jnp.sum(tile, axis=0, keepdims=True)
            left[c * tc + q, i] = tile.astype(jnp.bfloat16)
        degree = jnp.where(line == q, total, degree)
    xd[x] = degree
    pl.semaphore_wait(barrier, len(partners))

    def to_x(buf, sem):
        for k in range(1, nx):
            send(buf.at[x], buf.at[x], sem, k, x, *at_x(k))

    def from_x(buf, sem):
        for k in range(1, nx):
            other = wrap(x + k, nx)
            copy(buf.at[other], buf.at[other], sem, k, other, *at_x(k)).wait_recv()
        return sum(buf[k] for k in range(nx))

    def to_y(buf, sem):
        for k in range(1, ny):
            send(buf.at[y], buf.at[y], sem, k, y, *at_y(k))

    def from_y(buf, sem):
        for k in range(1, ny):
            other = wrap(y + k, ny)
            copy(buf.at[other], buf.at[other], sem, k, other, *at_y(k)).wait_recv()
        return sum(buf[k] for k in range(ny))

    to_x(xm, s_xm)
    to_x(xd, s_xd)
    for k in range(1, nx):
        other = wrap(x + k, nx)
        send(left.at[c * tc + other], stage.at[x], s_stage, k, x, *at_x(k))

    half = tc // 2

    def chunk(zz, cc, h):
        return left.at[pl.ds((zz * CORES + cc) * tc + h * half, half)]

    def ring_send(way, hop, h):
        part = chunk(wrap(z - way * (hop - 1), nz), core, h)
        sem = s_up if way == 1 else s_down
        n = (hop - 1) * 2 + h
        send(part, part, sem, n, n, r, wrap(z + way, nz) * CORES + core)

    def ring_wait(way, hop, h):
        part = chunk(wrap(z - way * hop, nz), core, h)
        sem = s_up if way == 1 else s_down
        n = (hop - 1) * 2 + h
        copy(part, part, sem, n, n, r, wrap(z - way, nz) * CORES + core).wait_recv()

    def hops(way, h):
        return nz // 2 if (way == 1) == (h == 0) else nz // 2 - 1

    def pair_send(away, h):
        part = chunk(wrap(z + away, nz), core, h)
        n = (away % nz) * 2 + h
        send(part, part, s_pair, n, n, r, z * CORES + 1 - core)

    def pair_wait(away, h):
        part = chunk(wrap(z + away, nz), 1 - core, h)
        n = (away % nz) * 2 + h
        copy(part, part, s_pair, n, n, r, z * CORES + 1 - core).wait_recv()

    def ring_pass(hop, h):
        for way in (1, -1):
            if hop <= hops(way, h):
                ring_wait(way, hop, h)
                if hop + 1 <= hops(way, h):
                    ring_send(way, hop + 1, h)
        for way in (1, -1):
            if hop <= hops(way, h):
                pair_send(-way * hop, h)

    for h in (0, 1):
        for way in (1, -1):
            ring_send(way, 1, h)
    for h in (0, 1):
        pair_send(0, h)
    stage[x] = left[c * tc + x]

    ym[y] = from_x(xm, s_xm)
    to_y(ym, s_ym)
    yd[y] = from_x(xd, s_xd)
    to_y(yd, s_yd)
    ring_pass(1, 0)

    marks = from_y(ym, s_ym)
    count = marks
    step = 1
    while step < rows * tr:
        count += jnp.where(lane >= step, pltpu.roll(count, step, 1), 0)
        step *= 2
    before = count - marks
    ids = jnp.zeros((SUBLANES, LANES), jnp.int32)
    for s in range(KEEP):
        hit = jnp.logical_and(marks == 1, before == s)
        ids = jnp.where(lane == s, jnp.sum(jnp.where(hit, lane, 0), axis=1, keepdims=True), ids)
    table[...] = ids
    fetch = pltpu.make_async_copy(table, slots, s_local.at[1])
    fetch.start()
    inverse = 1.0 / jnp.where(line < tc, from_y(yd, s_yd), 1.0)
    for q in range(tc):
        inv[c * tc + q] = inverse[q : q + 1]
    fetch.wait()

    for k in range(1, nx):
        other = wrap(x + k, nx)
        copy(stage.at[other], stage.at[other], s_stage, k, other, *at_x(k)).wait_recv()
    near = sorted(range(ny), key=lambda k: min(k, ny - k))
    for k in near:
        s = wrap(y + k, ny)
        t = jnp.clip(slots[x, s] - y * (nx * tr), 0, nx * tr - 1)
        tile = stage[lax.div(t, tr), lax.rem(t, tr)]
        if k == 0:
            cand[y] = tile
        else:
            cand_out[k] = tile
    for k in near[1:]:
        send(cand_out.at[k], cand.at[y], s_cand, k, y, *at_y(k))
    for k in range(1, cols):
        mine = inv.at[pl.ds(c * tc, tc)]
        send(mine, mine, s_inv, k, c, *at_col(k))

    ring_pass(1, 1)
    ring_pass(2, 0)
    ring_pass(2, 1)

    for k in near[1:]:
        other = wrap(y + k, ny)
        copy(cand.at[other], cand.at[other], s_cand, k, other, *at_y(k)).wait_recv()
    right[x * KEEP + y] = cand[lax.div(slots[x, y], nx * tr)]

    mine = right.at[x * KEEP + y]
    for k in near[1:]:
        send(mine, mine, s_gy, k, y, *at_y(k))

    def to_neighbours(i):
        part = right.at[x * KEEP + wrap(y + near[i], ny)]
        send(part, part, s_gxp, i, i, *at_x(1))
        send(part, part, s_gxm, i, i, *at_x(-1))

    def from_neighbours(i):
        s = wrap(y + near[i], ny)
        below = right.at[wrap(x - 1, nx) * KEEP + s]
        above = right.at[wrap(x + 1, nx) * KEEP + s]
        copy(below, below, s_gxp, i, i, *at_x(-1)).wait_recv()
        copy(above, above, s_gxm, i, i, *at_x(1)).wait_recv()
        if i % 2 == 0:
            send(below, below, s_rel, i, i, *at_x(1))
        else:
            send(above, above, s_rel, i, i, *at_x(-1))

    to_neighbours(0)
    ring_pass(3, 0)
    for i in range(1, ny):
        k = near[i]
        other = wrap(y + k, ny)
        part = right.at[x * KEEP + other]
        copy(part, part, s_gy, k, other, *at_y(k)).wait_recv()
        to_neighbours(i)
        if i >= 3:
            from_neighbours(i - 3)
        if i == 3:
            ring_pass(3, 1)
    for i in range(ny - 3, ny):
        from_neighbours(i)

    for hop in range(4, nz // 2 + 1):
        for h in (0, 1):
            ring_pass(hop, h)
    for away in range(nz):
        for h in (0, 1):
            pair_wait(away, h)
    for k in range(1, cols):
        other = wrap(c + k, cols)
        part = inv.at[pl.ds(other * tc, tc)]
        copy(part, part, s_inv, k, other, *at_col(k)).wait_recv()
    for q in range(tc):
        for s in range(KEEP):
            tile_row = slots[q, s]
            panel = left[tile_row].reshape(tr * size, size).astype(jnp.float32)
            wide[q, :, s * size : (s + 1) * size] = (panel * inv[tile_row]).astype(jnp.bfloat16)

    for i in range(ny):
        part = right.at[wrap(x + 2, nx) * KEEP + wrap(y + near[i], ny)]
        copy(part, part, s_rel, i, i, *at_x(-1 if i % 2 == 0 else 1)).wait_recv()

    mass = jnp.zeros((SUBLANES, LANES), jnp.float32)
    for q in range(tc):
        tiles = right[q * KEEP : (q + 1) * KEEP].reshape(KEEP * size, size)
        expanded = jnp.dot(wide[q], tiles, preferred_element_type=jnp.float32)
        expanded = expanded * inv[c * tc + q]
        square = expanded * expanded
        inflated[:, q * size : (q + 1) * size] = square
        mass = jnp.where(line == q, jnp.sum(square, axis=0, keepdims=True), mass)
    xs[x] = mass
    to_x(xs, s_xs)
    store = pltpu.make_async_copy(inflated, out_ref, s_local.at[2])
    store.start()
    ys[y] = from_x(xs, s_xs)
    to_y(ys, s_ys)
    nodes = rows * tr * size
    share = nodes / jnp.where(line < tc, from_y(ys, s_ys), 1.0)
    for q in range(tc):
        scale_ref[:, q * size : (q + 1) * size] = share[q : q + 1]
    store.wait()
    for made in sends:
        made.wait_send()


def on_device(weights, tile_mask):
    rows, cols = lax.axis_size("row"), lax.axis_size("col")
    tr, tc = tile_mask.shape
    height, width = weights.shape
    size = height // tr
    nx, ny, nz = CHIPS_X, rows // CHIPS_X, cols // CORES
    tiles = tc * cols
    f32, bf16, i32 = jnp.float32, jnp.bfloat16, jnp.int32
    vmem = pltpu.VMEM
    small = (SUBLANES, LANES)

    def pairs(n):
        return pltpu.SemaphoreType.DMA((2, n))

    inflated, scale = pl.pallas_call(
        functools.partial(kernel, size, rows, cols),
        out_shape=(
            jax.ShapeDtypeStruct((height, width), f32),
            jax.ShapeDtypeStruct((1, width), f32),
        ),
        in_specs=[
            pl.BlockSpec(memory_space=pltpu.SMEM),
            pl.BlockSpec(memory_space=pl.ANY),
        ],
        out_specs=(
            pl.BlockSpec(memory_space=pl.ANY),
            pl.BlockSpec(memory_space=vmem),
        ),
        scratch_shapes=[
            vmem((height, width), bf16),
            vmem((tiles, tr, size, size), bf16),
            vmem((nx, tr, size, size), bf16),
            vmem((ny, size, size), bf16),
            vmem((ny, size, size), bf16),
            vmem((tc * KEEP, size, size), bf16),
            vmem((tc, height, KEEP * size), bf16),
            vmem((height, width), f32),
            vmem((nx, *small), i32),
            vmem((nx, *small), f32),
            vmem((ny, *small), i32),
            vmem((ny, *small), f32),
            vmem((nx, *small), f32),
            vmem((ny, *small), f32),
            vmem((tiles, 1, size), f32),
            vmem(small, i32),
            pltpu.SMEM(small, i32),
            pairs(nx), pairs(nx), pairs(ny), pairs(ny), pairs(nx), pairs(ny),
            pairs(cols), pairs(nx), pairs(ny), pairs(ny),
            pairs(ny), pairs(ny), pairs(ny), pairs(nz), pairs(nz), pairs(2 * nz),
            pltpu.SemaphoreType.DMA((3,)),
        ],
        compiler_params=pltpu.CompilerParams(
            collective_id=0, has_side_effects=True, vmem_limit_bytes=32 * 1024 * 1024
        ),
        name="expand",
    )(tile_mask, weights)
    return inflated * scale


def solution(mesh):
    placed = (P("row", "col"), P("row", "col"))
    return jax.shard_map(
        on_device, mesh=mesh, in_specs=placed, out_specs=P("row", "col"), check_vma=False
    )
```

time: 134 us -> 60.6 us (0.45)
  the two profiles are of different devices: /device:TPU:448 before, /device:TPU:48 now
where the time goes in v1:
time: 60.6 us; the launch traced here: 60.5 us
  Pallas kernels  58 us (96%)
  local copies, waits for them, and re-layouts  1.63 us (3%)
  other arithmetic  0.86 us (1%)
    pallas_call x1, Pallas kernels, on_device(): pl.pallas_call(functools.partial(kernel, size, rows, cols), out_shape=(ja...  58 us
    unnamed x4, local copies, waits for them, and re-layouts  1.63 us

profile of v1, /device:TPU:48, one launch (start us, length us, event | category | flops | bytes accessed | tf_op | source)
XLA Modules:
  0.0 60.5 jit_solution(294553252213397748)
XLA Ops:
  0.0 0.0 copy-start
  0.0 0.9 %copy-done = bf16[256,512]{1,0:T(8,128)(2,1)S(1)} copy-done((bf16[256,512]{1,0:T(8,128)(2,1)S(1)}, bf16[256,512]{1,0:T(8,128)(2,1)}, u32[]{:S(2)}) %copy-start) | copy-done | bytes 262168
  1.0 0.0 copy-start.1
  1.0 0.7 %copy-done.1 = s32[2,4]{1,0:T(2,128)S(1)} copy-done((s32[2,4]{1,0:T(2,128)S(1)}, s32[2,4]{1,0:T(2,128)}, u32[]{:S(2)}) %copy-start.1) | copy-done | bytes 56
  1.6 58.0 %expand.1 = (f32[256,512]{1,0:T(8,128)S(1)}, f32[1,512]{1,0:T(1,128)S(1)}) custom-call(s32[2,4]{1,0:T(2,128)S(1)} %copy-done.1, bf16[256,512]{1,0:T(8,128)(2,1)S(1)} %copy-done), custom_call_target="tpu_custom_call" | custom-call | tf_op jit(solution)/shard_map/expand/pallas_call | solution.py:300
  59.6 0.9 %broadcast_multiply_fusion = f32[256,512]{1,0:T(8,128)} fusion(f32[256,512]{1,0:T(8,128)S(1)} %get-tuple-element.7, f32[512]{0:T(512)S(1)} %bitcast.1), kind=kLoop, calls=%fused_computation | loop fusion | flops 131072 | bytes 1050624 | tf_op jit(solution)/shard_map/mul | solution.py:342
Async XLA Ops:
  0.0 0.9 %copy-start = (bf16[256,512]{1,0:T(8,128)(2,1)S(1)}, bf16[256,512]{1,0:T(8,128)(2,1)}, u32[]{:S(2)}) copy-start(bf16[256,512]{1,0:T(8,128)(2,1)} %w_ref.1) | copy-start | bytes 786436
  1.0 0.7 %copy-start.1 = (s32[2,4]{1,0:T(2,128)S(1)}, s32[2,4]{1,0:T(2,128)}, u32[]{:S(2)}) copy-start(s32[2,4]{1,0:T(2,128)} %mask_ref.1) | copy-start | bytes 100

commit v2 on v1

v2 whole, which is shorter than its diff:
```python
import functools
import jax
import jax.numpy as jnp
from jax import lax
from jax.experimental import pallas as pl
from jax.experimental.pallas import tpu as pltpu
from jax.sharding import PartitionSpec as P

MESH = pl.DeviceIdType.MESH
KEEP = 8
CHIPS_X = 4
CORES = 2
SUBLANES, LANES = 8, 128


def kernel(
    size, rows, cols, mask_hbm, w_hbm, out_ref, scale_ref,
    mask_ref, block, left, stage, cand_out, cand, right, wide,
    xm, xd, ym, yd, xs, ys, inv, table, slots,
    s_xm, s_xd, s_ym, s_yd, s_xs, s_ys, s_inv, s_stage, s_cand, s_gy,
    s_gxp, s_gxm, s_rel, s_up, s_down, s_pair, s_local,
):
    nx, ny, nz = CHIPS_X, rows // CHIPS_X, cols // CORES
    tr, tc = block.shape[0] // size, block.shape[1] // size
    r, c = lax.axis_index("row"), lax.axis_index("col")
    x, y = lax.rem(r, nx), lax.div(r, nx)
    core, z = lax.rem(c, CORES), lax.div(c, CORES)
    column, h = lax.div(y, tr), lax.rem(y, tr)
    sends = []

    def wrap(a, n):
        return lax.rem(a + n, n)

    def copy(src, dst, sem, out, arrive, row, col):
        return pltpu.make_async_remote_copy(
            src_ref=src, dst_ref=dst, send_sem=sem.at[0, out], recv_sem=sem.at[1, arrive],
            device_id=(row, col), device_id_type=MESH,
        )

    def send(*args):
        made = copy(*args)
        made.start()
        sends.append(made)

    def at_x(k):
        return y * nx + wrap(x + k, nx), c

    def at_y(k):
        return wrap(y + k, ny) * nx + x, c

    def at_col(k):
        return r, wrap(c + k, cols)

    def at_owner(dx, dh):
        return (y - h + wrap(h + dh, tr)) * nx + wrap(x + dx, nx), c

    def slot(xx, yy):
        return lax.div(yy, tr) * KEEP + xx * tr + lax.rem(yy, tr)

    owners = [(dx, dh) for dx in range(nx) for dh in range(tr)]
    near = sorted(range(ny), key=lambda k: min(k, ny - k))
    far = near[:0:-1]

    barrier = pltpu.get_barrier_semaphore()
    partners = [at_x(k) for k in range(1, nx)] + [at_y(k) for k in range(1, ny)]
    partners += [at_col(k) for k in range(1, cols)]
    partners += [at_owner(dx, dh) for dx, dh in owners if dx and dh]
    for partner in partners:
        pl.semaphore_signal(barrier, inc=1, device_id=partner, device_id_type=MESH)

    fetch_mask = pltpu.make_async_copy(mask_hbm, mask_ref, s_local.at[1])
    fetch_mask.start()
    fetch = pltpu.make_async_copy(w_hbm, block, s_local.at[0])
    fetch.start()
    lane = lax.broadcasted_iota(jnp.int32, (SUBLANES, LANES), 1)
    line = lax.broadcasted_iota(jnp.int32, (SUBLANES, LANES), 0)
    xs[x] = jnp.zeros((SUBLANES, LANES), jnp.float32)
    fetch_mask.wait()
    own_mask = jnp.zeros((SUBLANES, LANES), jnp.int32)
    for i in range(tr):
        for q in range(tc):
            here = jnp.logical_and(lane == r * tr + i, line == q)
            own_mask = jnp.where(here, mask_ref[i, q], own_mask)
    ym[y] = own_mask
    fetch.wait()
    degree = jnp.zeros((SUBLANES, LANES), jnp.float32)
    for q in range(tc):
        total = jnp.zeros((1, size), jnp.float32)
        for i in range(tr):
            tile = block[i * size : (i + 1) * size, q * size : (q + 1) * size]
            tile = tile.astype(jnp.float32) * mask_ref[i, q].astype(jnp.float32)
            total += jnp.sum(tile, axis=0, keepdims=True)
            left[c * tc + q, i] = tile.astype(jnp.bfloat16)
        degree = jnp.where(line == q, total, degree)
    yd[y] = degree
    pl.semaphore_wait(barrier, len(partners))

    def to_x(buf, sem):
        for k in range(1, nx):
            send(buf.at[x], buf.at[x], sem, k, x, *at_x(k))

    def from_x(buf, sem):
        for k in range(1, nx):
            other = wrap(x + k, nx)
            copy(buf.at[other], buf.at[other], sem, k, other, *at_x(k)).wait_recv()
        return sum(buf[k] for k in range(nx))

    def to_y(buf, sem):
        for k in far:
            send(buf.at[y], buf.at[y], sem, k, y, *at_y(k))

    def from_y(buf, sem):
        for k in near[1:]:
            other = wrap(y + k, ny)
            copy(buf.at[other], buf.at[other], sem, k, other, *at_y(k)).wait_recv()
        return sum(buf[k] for k in range(ny))

    to_y(ym, s_ym)
    to_y(yd, s_yd)

    def chunk(zz, cc, g):
        return left.at[(zz * CORES + cc) * tc + g]

    def ring_send(way, hop, g):
        part = chunk(wrap(z - way * (hop - 1), nz), core, g)
        sem = s_up if way == 1 else s_down
        n = (hop - 1) * tc + g
        send(part, part, sem, n, n, r, wrap(z + way, nz) * CORES + core)

    def ring_wait(way, hop, g):
        part = chunk(wrap(z - way * hop, nz), core, g)
        sem = s_up if way == 1 else s_down
        n = (hop - 1) * tc + g
        copy(part, part, sem, n, n, r, wrap(z - way, nz) * CORES + core).wait_recv()

    def hops(way, g):
        return nz // 2 if (way == 1) == (g < tc // 2) else nz // 2 - 1

    def pair_send(away, g):
        part = chunk(wrap(z + away, nz), core, g)
        n = (away % nz) * tc + g
        send(part, part, s_pair, n, n, r, z * CORES + 1 - core)

    def pair_wait(away, g):
        part = chunk(wrap(z + away, nz), 1 - core, g)
        n = (away % nz) * tc + g
        copy(part, part, s_pair, n, n, r, z * CORES + 1 - core).wait_recv()

    def turn(way, g):
        return g if way == 1 else (g + tc // 2) % tc

    def ring_pass(hop, g):
        took = [(way, turn(way, g)) for way in (1, -1) if hop <= hops(way, turn(way, g))]
        for way, k in took:
            ring_wait(way, hop, k)
            if hop + 1 <= hops(way, k):
                ring_send(way, hop + 1, k)
        for way, k in took:
            pair_send(-way * hop, k)

    for g in range(tc):
        for way in (1, -1):
            ring_send(way, 1, turn(way, g))
    for k in far:
        other = wrap(y + k, ny)
        part = left.at[c * tc + lax.div(other, tr), lax.rem(other, tr)]
        send(part, stage.at[y], s_stage, k, y, *at_y(k))
    for g in range(tc):
        pair_send(0, g)
    stage[y] = left[c * tc + column, h]

    xm[x] = from_y(ym, s_ym)
    to_x(xm, s_xm)
    xd[x] = from_y(yd, s_yd)
    to_x(xd, s_xd)
    for g in range(tc - 1):
        ring_pass(1, g)

    marks = from_x(xm, s_xm)
    count = marks
    step = 1
    while step < rows * tr:
        count += jnp.where(lane >= step, pltpu.roll(count, step, 1), 0)
        step *= 2
    before = count - marks
    ids = jnp.zeros((SUBLANES, LANES), jnp.int32)
    for s in range(KEEP):
        hit = jnp.logical_and(marks == 1, before == s)
        ids = jnp.where(lane == s, jnp.sum(jnp.where(hit, lane, 0), axis=1, keepdims=True), ids)
    table[...] = ids
    fetch = pltpu.make_async_copy(table, slots, s_local.at[1])
    fetch.start()
    inverse = 1.0 / jnp.where(line < tc, from_x(xd, s_xd), 1.0)
    for q in range(tc):
        inv[c * tc + q] = inverse[q : q + 1]
    for k in near[1:]:
        other = wrap(y + k, ny)
        copy(stage.at[other], stage.at[other], s_stage, k, other, *at_y(k)).wait_recv()
    fetch.wait()

    me = x * tr + h
    for n, (dx, dh) in enumerate(owners):
        s = wrap(x + dx, nx) * tr + wrap(h + dh, tr)
        tile = stage[lax.div(slots[column, s], nx * tr)]
        if n == 0:
            cand[me] = tile
        else:
            cand_out[n] = tile
    order = sorted(range(1, len(owners)), key=lambda n: -min(owners[n][0], nx - owners[n][0]))
    for n in order:
        send(cand_out.at[n], cand.at[me], s_cand, n, me, *at_owner(*owners[n]))
    for k in range(1, cols):
        mine = inv.at[pl.ds(c * tc, tc)]
        send(mine, mine, s_inv, k, c, *at_col(k))

    ring_pass(1, tc - 1)
    for g in range(tc):
        ring_pass(2, g)

    for n in order:
        dx, dh = owners[n]
        other = wrap(x + dx, nx) * tr + wrap(h + dh, tr)
        copy(cand.at[other], cand.at[other], s_cand, n, other, *at_owner(dx, dh)).wait_recv()
    right[slot(x, y)] = cand[lax.rem(slots[column, me], nx * tr)]

    mine = right.at[slot(x, y)]
    for k in near[1:]:
        send(mine, mine, s_gy, k, y, *at_y(k))

    def to_neighbours(i):
        part = right.at[slot(x, wrap(y + near[i], ny))]
        send(part, part, s_gxp, i, i, *at_x(1))
        send(part, part, s_gxm, i, i, *at_x(-1))

    def from_neighbours(i):
        other = wrap(y + near[i], ny)
        below = right.at[slot(wrap(x - 1, nx), other)]
        above = right.at[slot(wrap(x + 1, nx), other)]
        copy(below, below, s_gxp, i, i, *at_x(-1)).wait_recv()
        copy(above, above, s_gxm, i, i, *at_x(1)).wait_recv()
        if i % 2 == 0:
            send(below, below, s_rel, i, i, *at_x(1))
        else:
            send(above, above, s_rel, i, i, *at_x(-1))

    to_neighbours(0)
    ring_pass(3, 0)
    ring_pass(3, 1)
    for i in range(1, ny):
        k = near[i]
        other = wrap(y + k, ny)
        part = right.at[slot(x, other)]
        copy(part, part, s_gy, k, other, *at_y(k)).wait_recv()
        to_neighbours(i)
        if i >= 3:
            from_neighbours(i - 3)
        if i in (2, 3):
            ring_pass(3, i)
    for i in range(ny - 3, ny):
        from_neighbours(i)

    for hop in range(4, nz // 2 + 1):
        for g in range(tc):
            ring_pass(hop, g)
    for away in range(nz):
        for g in range(tc):
            pair_wait(away, g)
    for k in range(1, cols):
        other = wrap(c + k, cols)
        part = inv.at[pl.ds(other * tc, tc)]
        copy(part, part, s_inv, k, other, *at_col(k)).wait_recv()
    for q in range(tc):
        for s in range(KEEP):
            tile_row = slots[q, s]
            panel = left[tile_row].reshape(tr * size, size).astype(jnp.float32)
            wide[q, :, s * size : (s + 1) * size] = (panel * inv[tile_row]).astype(jnp.bfloat16)

    for i in range(ny):
        part = right.at[slot(wrap(x + 2, nx), wrap(y + near[i], ny))]
        copy(part, part, s_rel, i, i, *at_x(-1 if i % 2 == 0 else 1)).wait_recv()

    mass = jnp.zeros((SUBLANES, LANES), jnp.float32)
    for q in range(tc):
        tiles = right[q * KEEP : (q + 1) * KEEP].reshape(KEEP * size, size)
        expanded = jnp.dot(wide[q], tiles, preferred_element_type=jnp.float32)
        expanded = expanded * inv[c * tc + q]
        square = expanded * expanded
        out_ref[:, q * size : (q + 1) * size] = square
        mass = jnp.where(line == q, jnp.sum(square, axis=0, keepdims=True), mass)
    xs[x] = mass
    to_x(xs, s_xs)
    ys[y] = from_x(xs, s_xs)
    to_y(ys, s_ys)
    nodes = rows * tr * size
    share = nodes / jnp.where(line < tc, from_y(ys, s_ys), 1.0)
    for q in range(tc):
        scale_ref[:, q * size : (q + 1) * size] = share[q : q + 1]
    for made in sends:
        made.wait_send()


def on_device(weights, tile_mask):
    rows, cols = lax.axis_size("row"), lax.axis_size("col")
    tr, tc = tile_mask.shape
    height, width = weights.shape
    size = height // tr
    nx, ny, nz = CHIPS_X, rows // CHIPS_X, cols // CORES
    tiles = tc * cols
    f32, bf16, i32 = jnp.float32, jnp.bfloat16, jnp.int32
    vmem = pltpu.VMEM
    small = (SUBLANES, LANES)

    def pairs(n):
        return pltpu.SemaphoreType.DMA((2, n))

    inflated, scale = pl.pallas_call(
        functools.partial(kernel, size, rows, cols),
        out_shape=(
            jax.ShapeDtypeStruct((height, width), f32),
            jax.ShapeDtypeStruct((1, width), f32),
        ),
        in_specs=[
            pl.BlockSpec(memory_space=pltpu.HBM),
            pl.BlockSpec(memory_space=pltpu.HBM),
        ],
        out_specs=(
            pl.BlockSpec(memory_space=vmem),
            pl.BlockSpec(memory_space=vmem),
        ),
        scratch_shapes=[
            pltpu.SMEM((tr, tc), i32),
            vmem((height, width), bf16),
            vmem((tiles, tr, size, size), bf16),
            vmem((ny, size, size), bf16),
            vmem((ny, size, size), bf16),
            vmem((ny, size, size), bf16),
            vmem((tc * KEEP, size, size), bf16),
            vmem((tc, height, KEEP * size), bf16),
            vmem((nx, *small), i32),
            vmem((nx, *small), f32),
            vmem((ny, *small), i32),
            vmem((ny, *small), f32),
            vmem((nx, *small), f32),
            vmem((ny, *small), f32),
            vmem((tiles, 1, size), f32),
            vmem(small, i32),
            pltpu.SMEM(small, i32),
            pairs(nx), pairs(nx), pairs(ny), pairs(ny), pairs(nx), pairs(ny),
            pairs(cols), pairs(ny), pairs(KEEP), pairs(ny),
            pairs(ny), pairs(ny), pairs(ny), pairs(tc * nz // 2), pairs(tc * nz // 2),
            pairs(tc * nz),
            pltpu.SemaphoreType.DMA((2,)),
        ],
        compiler_params=pltpu.CompilerParams(
            collective_id=0, has_side_effects=True, vmem_limit_bytes=32 * 1024 * 1024
        ),
        name="expand",
    )(
        pltpu.with_memory_space_constraint(tile_mask, pltpu.HBM),
        pltpu.with_memory_space_constraint(weights, pltpu.HBM),
    )
    return inflated * scale


def solution(mesh):
    placed = (P("row", "col"), P("row", "col"))
    return jax.shard_map(
        on_device, mesh=mesh, in_specs=placed, out_specs=P("row", "col"), check_vma=False
    )
```

time: 60.6 us -> 58.4 us (0.964)
  the two profiles are of different devices: /device:TPU:48 before, /device:TPU:8 now
where the time goes in v2:
time: 58.4 us; the launch traced here: 58.3 us
  Pallas kernels  57.4 us (98%)
  other arithmetic  0.86 us (1%)
    pallas_call x1, Pallas kernels, on_device(): pl.pallas_call(functools.partial(kernel, size, rows, cols), out_shape=(ja...  57.4 us

profile of v2, /device:TPU:8, one launch (start us, length us, event | category | flops | bytes accessed | tf_op | source)
XLA Modules:
  0.0 58.3 jit_solution(2450053757773163451)
XLA Ops:
  0.0 57.4 %expand.1 = (f32[256,512]{1,0:T(8,128)S(1)}, f32[1,512]{1,0:T(1,128)S(1)}) custom-call(s32[2,4]{1,0:T(2,128)} %mask_hbm.1, bf16[256,512]{1,0:T(8,128)(2,1)} %w_hbm.1), custom_call_target="tpu_custom_call" | custom-call | tf_op jit(solution)/shard_map/expand/pallas_call | solution.py:316
  57.4 0.9 %broadcast_multiply_fusion = f32[256,512]{1,0:T(8,128)} fusion(f32[256,512]{1,0:T(8,128)S(1)} %get-tuple-element.7, f32[512]{0:T(512)S(1)} %bitcast.1), kind=kLoop, calls=%fused_computation | loop fusion | flops 131072 | bytes 1050624 | tf_op jit(solution)/shard_map/mul | solution.py:362

commit v3 on v2

--- a/solution.py
+++ b/solution.py
@@ -18,7 +18,7 @@
     mask_ref, block, left, stage, cand_out, cand, right, wide,
     xm, xd, ym, yd, xs, ys, inv, table, slots,
     s_xm, s_xd, s_ym, s_yd, s_xs, s_ys, s_inv, s_stage, s_cand, s_gy,
-    s_gxp, s_gxm, s_rel, s_up, s_down, s_pair, s_local,
+    s_gx, s_next, s_up, s_down, s_pair, s_local,
 ):
     nx, ny, nz = CHIPS_X, rows // CHIPS_X, cols // CORES
     tr, tc = block.shape[0] // size, block.shape[1] // size
@@ -214,7 +214,7 @@
         send(mine, mine, s_inv, k, c, *at_col(k))
 
     ring_pass(1, tc - 1)
-    for g in range(tc):
+    for g in range(tc - 1):
         ring_pass(2, g)
 
     for n in order:
@@ -223,41 +223,39 @@
         copy(cand.at[other], cand.at[other], s_cand, n, other, *at_owner(dx, dh)).wait_recv()
     right[slot(x, y)] = cand[lax.rem(slots[column, me], nx * tr)]
 
+    beside = (1, ny - 1)
+    spread = sorted(near[1:], key=lambda k: (k in beside, min(k, ny - k)))
     mine = right.at[slot(x, y)]
-    for k in near[1:]:
+
+    def to_others(k):
+        part = right.at[slot(x, wrap(y + k, ny))]
+        for j in (2, 1, 3):
+            send(part, part, s_gx, j * ny + k, j * ny + k, *at_x(j))
+
+    def from_others(k):
+        for j in range(1, nx):
+            part = right.at[slot(wrap(x - j, nx), wrap(y + k, ny))]
+            copy(part, part, s_gx, j * ny + k, j * ny + k, *at_x(-j)).wait_recv()
+
+    to_others(0)
+    for k in spread:
         send(mine, mine, s_gy, k, y, *at_y(k))
-
-    def to_neighbours(i):
-        part = right.at[slot(x, wrap(y + near[i], ny))]
-        send(part, part, s_gxp, i, i, *at_x(1))
-        send(part, part, s_gxm, i, i, *at_x(-1))
-
-    def from_neighbours(i):
-        other = wrap(y + near[i], ny)
-        below = right.at[slot(wrap(x - 1, nx), other)]
-        above = right.at[slot(wrap(x + 1, nx), other)]
-        copy(below, below, s_gxp, i, i, *at_x(-1)).wait_recv()
-        copy(above, above, s_gxm, i, i, *at_x(1)).wait_recv()
-        if i % 2 == 0:
-            send(below, below, s_rel, i, i, *at_x(1))
-        else:
-            send(above, above, s_rel, i, i, *at_x(-1))
-
-    to_neighbours(0)
+    ring_pass(2, tc - 1)
     ring_pass(3, 0)
-    ring_pass(3, 1)
-    for i in range(1, ny):
-        k = near[i]
+    for n, k in enumerate(spread):
         other = wrap(y + k, ny)
         part = right.at[slot(x, other)]
         copy(part, part, s_gy, k, other, *at_y(k)).wait_recv()
-        to_neighbours(i)
-        if i >= 3:
-            from_neighbours(i - 3)
-        if i in (2, 3):
-            ring_pass(3, i)
-    for i in range(ny - 3, ny):
-        from_neighbours(i)
+        if k not in beside:
+            to_others(k)
+        if n == 1:
+            from_others(0)
+            for j in range(1, nx):
+                part = right.at[slot(wrap(x - j, nx), y)]
+                for way, to in enumerate((1, -1)):
+                    send(part, part, s_next, j * 2 + way, j * 2 + way, *at_y(to))
+        if n in (0, 2, 4):
+            ring_pass(3, n // 2 + 1)
 
     for hop in range(4, nz // 2 + 1):
         for g in range(tc):
@@ -275,9 +273,13 @@
             panel = left[tile_row].reshape(tr * size, size).astype(jnp.float32)
             wide[q, :, s * size : (s + 1) * size] = (panel * inv[tile_row]).astype(jnp.bfloat16)
 
-    for i in range(ny):
-        part = right.at[slot(wrap(x + 2, nx), wrap(y + near[i], ny))]
-        copy(part, part, s_rel, i, i, *at_x(-1 if i % 2 == 0 else 1)).wait_recv()
+    for k in range(1, nx):
+        for way, to in enumerate((1, -1)):
+            part = right.at[slot(wrap(x - k, nx), wrap(y - to, ny))]
+            copy(part, part, s_next, k * 2 + way, k * 2 + way, *at_y(-to)).wait_recv()
+    for k in spread:
+        if k not in beside:
+            from_others(k)
 
     mass = jnp.zeros((SUBLANES, LANES), jnp.float32)
     for q in range(tc):
@@ -347,7 +349,7 @@
             pltpu.SMEM(small, i32),
             pairs(nx), pairs(nx), pairs(ny), pairs(ny), pairs(nx), pairs(ny),
             pairs(cols), pairs(ny), pairs(KEEP), pairs(ny),
-            pairs(ny), pairs(ny), pairs(ny), pairs(tc * nz // 2), pairs(tc * nz // 2),
+            pairs(nx * ny), pairs(2 * nx), pairs(tc * nz // 2), pairs(tc * nz // 2),
             pairs(tc * nz),
             pltpu.SemaphoreType.DMA((2,)),
         ],

time: 58.4 us -> 53.1 us (0.909)
  the two profiles are of different devices: /device:TPU:8 before, /device:TPU:1 now
where the time goes in v3:
time: 53.1 us; the launch traced here: 52.8 us
  Pallas kernels  51.9 us (98%)
  other arithmetic  0.86 us (2%)
    pallas_call x1, Pallas kernels, on_device(): pl.pallas_call(functools.partial(kernel, size, rows, cols), out_shape=(ja...  51.9 us

profile of v3, /device:TPU:1, one launch (start us, length us, event | category | flops | bytes accessed | tf_op | source)
XLA Modules:
  0.0 52.8 jit_solution(2719175947022392482)
XLA Ops:
  0.0 51.9 %expand.1 = (f32[256,512]{1,0:T(8,128)S(1)}, f32[1,512]{1,0:T(1,128)S(1)}) custom-call(s32[2,4]{1,0:T(2,128)} %mask_hbm.1, bf16[256,512]{1,0:T(8,128)(2,1)} %w_hbm.1), custom_call_target="tpu_custom_call" | custom-call | tf_op jit(solution)/shard_map/expand/pallas_call | solution.py:318
  51.9 0.9 %broadcast_multiply_fusion = f32[256,512]{1,0:T(8,128)} fusion(f32[256,512]{1,0:T(8,128)S(1)} %get-tuple-element.7, f32[512]{0:T(512)S(1)} %bitcast.1), kind=kLoop, calls=%fused_computation | loop fusion | flops 131072 | bytes 1050624 | tf_op jit(solution)/shard_map/mul | solution.py:364

commit v4 on v3

--- a/solution.py
+++ b/solution.py
@@ -16,8 +16,8 @@
 def kernel(
     size, rows, cols, mask_hbm, w_hbm, out_ref, scale_ref,
     mask_ref, block, left, stage, cand_out, cand, right, wide,
-    xm, xd, ym, yd, xs, ys, inv, table, slots,
-    s_xm, s_xd, s_ym, s_yd, s_xs, s_ys, s_inv, s_stage, s_cand, s_gy,
+    xm, xd, ym, yd, rs, inv, table, slots,
+    s_xm, s_xd, s_ym, s_yd, s_rs, s_inv, s_stage, s_cand, s_gy,
     s_gx, s_next, s_up, s_down, s_pair, s_local,
 ):
     nx, ny, nz = CHIPS_X, rows // CHIPS_X, cols // CORES
@@ -51,6 +51,9 @@
     def at_col(k):
         return r, wrap(c + k, cols)
 
+    def at_row(dx, dy):
+        return wrap(y + dy, ny) * nx + wrap(x + dx, nx), c
+
     def at_owner(dx, dh):
         return (y - h + wrap(h + dh, tr)) * nx + wrap(x + dx, nx), c
 
@@ -58,6 +61,8 @@
         return lax.div(yy, tr) * KEEP + xx * tr + lax.rem(yy, tr)
 
     owners = [(dx, dh) for dx in range(nx) for dh in range(tr)]
+    others = [(dx, dy) for dx in range(nx) for dy in range(ny) if dx or dy]
+    others.sort(key=lambda o: -min(o[0], nx - o[0]) - min(o[1], ny - o[1]))
     near = sorted(range(ny), key=lambda k: min(k, ny - k))
     far = near[:0:-1]
 
@@ -74,7 +79,6 @@
     fetch.start()
     lane = lax.broadcasted_iota(jnp.int32, (SUBLANES, LANES), 1)
     line = lax.broadcasted_iota(jnp.int32, (SUBLANES, LANES), 0)
-    xs[x] = jnp.zeros((SUBLANES, LANES), jnp.float32)
     fetch_mask.wait()
     own_mask = jnp.zeros((SUBLANES, LANES), jnp.int32)
     for i in range(tr):
@@ -289,12 +293,14 @@
         square = expanded * expanded
         out_ref[:, q * size : (q + 1) * size] = square
         mass = jnp.where(line == q, jnp.sum(square, axis=0, keepdims=True), mass)
-    xs[x] = mass
-    to_x(xs, s_xs)
-    ys[y] = from_x(xs, s_xs)
-    to_y(ys, s_ys)
+    rs[r] = mass[:tc]
+    for n, (dx, dy) in enumerate(others):
+        send(rs.at[r], rs.at[r], s_rs, n, n, *at_row(dx, dy))
+    for n, (dx, dy) in enumerate(others):
+        other, col = at_row(nx - dx, ny - dy)
+        copy(rs.at[other], rs.at[other], s_rs, n, n, other, col).wait_recv()
     nodes = rows * tr * size
-    share = nodes / jnp.where(line < tc, from_y(ys, s_ys), 1.0)
+    share = nodes / sum(rs[k] for k in range(rows))
     for q in range(tc):
         scale_ref[:, q * size : (q + 1) * size] = share[q : q + 1]
     for made in sends:
@@ -342,12 +348,11 @@
             vmem((nx, *small), f32),
             vmem((ny, *small), i32),
             vmem((ny, *small), f32),
-            vmem((nx, *small), f32),
-            vmem((ny, *small), f32),
+            vmem((rows, tc, size), f32),
             vmem((tiles, 1, size), f32),
             vmem(small, i32),
             pltpu.SMEM(small, i32),
-            pairs(nx), pairs(nx), pairs(ny), pairs(ny), pairs(nx), pairs(ny),
+            pairs(nx), pairs(nx), pairs(ny), pairs(ny), pairs(rows),
             pairs(cols), pairs(ny), pairs(KEEP), pairs(ny),
             pairs(nx * ny), pairs(2 * nx), pairs(tc * nz // 2), pairs(tc * nz // 2),
             pairs(tc * nz),

time: 53.1 us -> 52.1 us (0.981)
  Pallas kernels: 51.9 us -> 51.1 us
    pallas_call x1, Pallas kernels: 51.9 us -> 51.1 us  [on_device(): pl.pallas_call(functools.partial(kernel, size, rows, cols), out_shape=(ja...]
where the time goes in v4:
time: 52.1 us; the launch traced here: 52 us
  Pallas kernels  51.1 us (98%)
  other arithmetic  0.86 us (2%)
    pallas_call x1, Pallas kernels, on_device(): pl.pallas_call(functools.partial(kernel, size, rows, cols), out_shape=(ja...  51.1 us

profile of v4, /device:TPU:1, one launch (start us, length us, event | category | flops | bytes accessed | tf_op | source)
XLA Modules:
  0.0 52.0 jit_solution(16989950431080360866)
XLA Ops:
  0.0 51.1 %expand.1 = (f32[256,512]{1,0:T(8,128)S(1)}, f32[1,512]{1,0:T(1,128)S(1)}) custom-call(s32[2,4]{1,0:T(2,128)} %mask_hbm.1, bf16[256,512]{1,0:T(8,128)(2,1)} %w_hbm.1), custom_call_target="tpu_custom_call" | custom-call | tf_op jit(solution)/shard_map/expand/pallas_call | solution.py:324
  51.1 0.9 %broadcast_multiply_fusion = f32[256,512]{1,0:T(8,128)} fusion(f32[256,512]{1,0:T(8,128)S(1)} %get-tuple-element.7, f32[512]{0:T(512)S(1)} %bitcast.1), kind=kLoop, calls=%fused_computation | loop fusion | flops 131072 | bytes 1050624 | tf_op jit(solution)/shard_map/mul | solution.py:369

commit v5 on v4

--- a/solution.py
+++ b/solution.py
@@ -296,6 +296,8 @@
     rs[r] = mass[:tc]
     for n, (dx, dy) in enumerate(others):
         send(rs.at[r], rs.at[r], s_rs, n, n, *at_row(dx, dy))
+    for made in sends:
+        made.wait_send()
     for n, (dx, dy) in enumerate(others):
         other, col = at_row(nx - dx, ny - dy)
         copy(rs.at[other], rs.at[other], s_rs, n, n, other, col).wait_recv()
@@ -303,8 +305,6 @@
     share = nodes / sum(rs[k] for k in range(rows))
     for q in range(tc):
         scale_ref[:, q * size : (q + 1) * size] = share[q : q + 1]
-    for made in sends:
-        made.wait_send()
 
 
 def on_device(weights, tile_mask):

time: 52.1 us -> 51.8 us (level)
  no operation moved by 1% of the time
where the time goes in v5:
time: 51.8 us; the launch traced here: 51.7 us
  Pallas kernels  50.8 us (98%)
  other arithmetic  0.86 us (2%)
    pallas_call x1, Pallas kernels, on_device(): pl.pallas_call(functools.partial(kernel, size, rows, cols), out_shape=(ja...  50.8 us

profile of v5, /device:TPU:1, one launch (start us, length us, event | category | flops | bytes accessed | tf_op | source)
XLA Modules:
  0.0 51.7 jit_solution(15972971595829222308)
XLA Ops:
  0.0 50.8 %expand.1 = (f32[256,512]{1,0:T(8,128)S(1)}, f32[1,512]{1,0:T(1,128)S(1)}) custom-call(s32[2,4]{1,0:T(2,128)} %mask_hbm.1, bf16[256,512]{1,0:T(8,128)(2,1)} %w_hbm.1), custom_call_target="tpu_custom_call" | custom-call | tf_op jit(solution)/shard_map/expand/pallas_call | solution.py:324
  50.8 0.9 %broadcast_multiply_fusion = f32[256,512]{1,0:T(8,128)} fusion(f32[256,512]{1,0:T(8,128)S(1)} %get-tuple-element.7, f32[512]{0:T(512)S(1)} %bitcast.1), kind=kLoop, calls=%fused_computation | loop fusion | flops 131072 | bytes 1050624 | tf_op jit(solution)/shard_map/mul | solution.py:369

commit v6 on v5

--- a/solution.py
+++ b/solution.py
@@ -10,7 +10,7 @@
 KEEP = 8
 CHIPS_X = 4
 CORES = 2
-SUBLANES, LANES = 8, 128
+SUBLANES, LANES = 4, 128
 
 
 def kernel(

time: 51.8 us -> 51.7 us (level)
  Pallas kernels: 50.8 us -> 50.2 us
    pallas_call x1, Pallas kernels: 50.8 us -> 50.2 us  [on_device(): pl.pallas_call(functools.partial(kernel, size, rows, cols), out_shape=(ja...]
where the time goes in v6:
time: 51.7 us; the launch traced here: 51.1 us
  Pallas kernels  50.2 us (97%)
  other arithmetic  0.86 us (2%)
    pallas_call x1, Pallas kernels, on_device(): pl.pallas_call(functools.partial(kernel, size, rows, cols), out_shape=(ja...  50.2 us

profile of v6, /device:TPU:1, one launch (start us, length us, event | category | flops | bytes accessed | tf_op | source)
XLA Modules:
  0.0 51.1 jit_solution(5617910172341071179)
XLA Ops:
  0.0 50.2 %expand.1 = (f32[256,512]{1,0:T(8,128)S(1)}, f32[1,512]{1,0:T(1,128)S(1)}) custom-call(s32[2,4]{1,0:T(2,128)} %mask_hbm.1, bf16[256,512]{1,0:T(8,128)(2,1)} %w_hbm.1), custom_call_target="tpu_custom_call" | custom-call | tf_op jit(solution)/shard_map/expand/pallas_call | solution.py:324
  50.2 0.9 %broadcast_multiply_fusion = f32[256,512]{1,0:T(8,128)} fusion(f32[256,512]{1,0:T(8,128)S(1)} %get-tuple-element.7, f32[512]{0:T(512)S(1)} %bitcast.1), kind=kLoop, calls=%fused_computation | loop fusion | flops 131072 | bytes 1050624 | tf_op jit(solution)/shard_map/mul | solution.py:369
